TPU v7x, 256 devices: a whole 4x4x8 slice. The times are simulated.
256 devices in a mesh: batch: 16 (over z, core), vocab: 16 (over y, x).
Axes of the slice: x: 4, y: 4, z: 8, core: 2. Of those that a mesh axis runs over, the one named last changes fastest.
Arguments:
- hidden: bfloat16 [2048, 4096], P('batch'), may hold values from -40 to 40
- exit_layer: int32 [2048], P('batch'), may hold values from 0 to 7
- exit_gains: float32 [8, 4096], replicated, may hold values from 0.1 to 1.9
- unembed: bfloat16 [4096, 128256], P(None, ('batch', 'vocab')), may hold values from -10 to 10
- targets: int32 [2048], replicated, may hold values from 0 to 128255
- values: float32 [2048], P('batch'), may hold values from -6 to 6
- rewards: float32 [2048], P('batch'), may hold values from -2 to 2
- ref_logprob: float32 [2048], P('batch'), may hold values from -16 to -6
- segment_end: int32 [2048], P('batch'), may hold values 0 or 1
Outputs:
- logprob: float32 [2048], P('batch')
- advantages: float32 [2048], P('batch')
All inputs are finite; a program needn't handle non-finite values. No bound on the sum of `segment_end` on one device may be relied on, other than what follows from the above.
Results may differ from a plain program's by a relative error of at most 0.00054.
Values may be sent and summed in bfloat16 or wider, within the bound.
A program may use at most 128 MiB of HBM per device.

v0:
```python
import jax
import jax.numpy as jnp
from jax import lax
from jax.sharding import Mesh
from jax.sharding import PartitionSpec as P

BATCH_VOCAB = ("batch", "vocab_0", "vocab_1")
VOCAB = ("vocab_0", "vocab_1")
epsilon_norm = 1e-05
discount = 1.0
trace_decay = 0.999
penalty_weight = 0.1


def gathered_once(shard, axis):
    leaves = jax.tree.leaves(shard)
    sequence = sorted(range(len(leaves)), key=lambda k: -leaves[k].size)
    width = (1, *leaves[sequence[0]].shape)[-1]
    lines = [
        jnp.pad(leaves[k].reshape(-1), (0, -leaves[k].size % width)).reshape(-1, width)
        for k in sequence
    ]
    both, at, found = (lax.all_gather(jnp.concatenate(lines), axis), 0, {})
    for k, line in zip(sequence, lines):
        piece = both[:, at : at + len(line)].reshape(len(both), -1)
        found[k] = piece[:, : leaves[k].size].reshape(-1, *leaves[k].shape)
        at += len(line)
    numbers = iter(range(len(leaves)))
    return jax.tree.map(lambda _: found[next(numbers)], shard)


def joined_all(shard, axes, combine):
    for axis in axes:
        pieces = gathered_once(shard, axis)
        shard = jax.tree.map(lambda part: part[0], pieces)
        for k in range(1, lax.axis_size(axis)):
            shard = combine(shard, jax.tree.map(lambda part: part[k], pieces))
    return shard


def from_behind(value, axis, steps):
    count = lax.axis_size(axis)
    initial, last = (max(0, -steps), min(count, count - steps))
    return lax.ppermute(value, axis, [(source, source + steps) for source in range(initial, last)])


def from_everyone(shard, axis):
    length = lax.axis_size(axis)
    return lax.all_to_all(
        jnp.broadcast_to(shard[None], (length, *shard.shape)), axis, 0, 0, tiled=True
    )


def gathered_once_2(shard, axis):
    leaves = jax.tree.leaves(shard)
    sequence = sorted(range(len(leaves)), key=lambda k: -leaves[k].size)
    width = (1, *leaves[sequence[0]].shape)[-1]
    lines = [
        jnp.pad(leaves[k].reshape(-1), (0, -leaves[k].size % width)).reshape(-1, width)
        for k in sequence
    ]
    both, at, found = (from_everyone(jnp.concatenate(lines), axis), 0, {})
    for k, line in zip(sequence, lines):
        piece = both[:, at : at + len(line)].reshape(len(both), -1)
        found[k] = piece[:, : leaves[k].size].reshape(-1, *leaves[k].shape)
        at += len(line)
    numbers = iter(range(len(leaves)))
    return jax.tree.map(lambda _: found[next(numbers)], shard)


def collected_alike(shard, axis):
    leaves, found = (jax.tree.leaves(shard), {})
    for initial, a in enumerate(leaves):
        if initial not in found:
            alike = [k for k, b in enumerate(leaves) if b.dtype == a.dtype]
            got = (
                gathered_once_2([leaves[k] for k in alike], axis)
                if len(alike) > 1
                else [from_everyone(a, axis)]
            )
            for k, b in zip(alike, got):
                found[k] = b
    numbers = iter(range(len(leaves)))
    return jax.tree.map(lambda _: found[next(numbers)], shard)


def joined_by_halves(pieces, combine):
    while len(jax.tree.leaves(pieces)[0]) > 1:
        pieces = jax.vmap(combine)(
            *(jax.tree.map(lambda part: part[side::2], pieces) for side in (0, 1))
        )
    return jax.tree.map(lambda part: part[0], pieces)


def prefix(shard, axis, combine, identity):
    length, mine = (lax.axis_size(axis), lax.axis_index(axis))
    passed = jnp.arange(length) > mine

    def kept(part, zero, own):
        part = jnp.where(
            passed.reshape(-1, *(1 for _ in own.shape)), part, jnp.asarray(zero, own.dtype)
        )
        return part[::-1]

    pieces = collected_alike(shard, axis)
    return joined_by_halves(jax.tree.map(kept, pieces, identity, shard), combine)


def normalize(rows, layers, exit_gains):
    states = rows.astype(jnp.float32)
    inverse = lax.rsqrt(jnp.mean(states * states, axis=-1, keepdims=True) + epsilon_norm)
    selector = (
        layers[:, None] == jnp.arange(exit_gains.shape[0], dtype=jnp.int32)[None, :]
    ).astype(jnp.float32)
    scaling = jnp.dot(selector, exit_gains, precision=lax.Precision.HIGHEST)
    return (states * inverse * scaling).astype(jnp.bfloat16)


def per_device(
    hidden, exit_layer, exit_gains, unembed, targets, values, rewards, ref_logprob, segment_end
):
    column_count = unembed.shape[1]
    column_start = lax.axis_index(BATCH_VOCAB) * column_count
    columns = jnp.arange(column_count, dtype=jnp.int32)
    total_rows = targets.shape[0]
    owned = hidden.shape[0]
    peers = lax.axis_size("batch")
    width = hidden.shape[1]
    share = owned // lax.axis_size(VOCAB)
    first_row = lax.axis_index(VOCAB) * share
    own_rows = lax.dynamic_slice_in_dim(hidden, first_row, share, 0)
    own_layers = lax.dynamic_slice_in_dim(exit_layer, first_row, share, 0)
    normed = normalize(own_rows, own_layers, exit_gains)
    gathered = lax.all_gather(normed, BATCH_VOCAB, axis=0, tiled=True)
    block_rows = 512
    block_count = total_rows // block_rows

    def score_block(pair):
        rows_block, ids_block = pair
        logits = jnp.dot(rows_block, unembed, preferred_element_type=jnp.float32)
        row_max = jnp.max(logits, axis=1)
        row_total = jnp.sum(jnp.exp(logits - row_max[:, None]), axis=1)
        wanted = ids_block - column_start
        picked = jnp.sum(jnp.where(columns[None, :] == wanted[:, None], logits, 0.0), axis=1)
        return (row_max, row_total, picked)

    maxima, totals, picks = lax.map(
        score_block,
        (
            gathered.reshape(block_count, block_rows, width),
            targets.reshape(block_count, block_rows),
        ),
    )
    maxima = maxima.reshape(total_rows)
    totals = totals.reshape(total_rows)
    picks = picks.reshape(total_rows)
    maxima, totals, picks = (
        lax.all_to_all(maxima, "batch", split_axis=0, concat_axis=0, tiled=True),
        lax.all_to_all(totals, "batch", split_axis=0, concat_axis=0, tiled=True),
        lax.all_to_all(picks, "batch", split_axis=0, concat_axis=0, tiled=True),
    )
    maxima = maxima.reshape(peers, owned)
    totals = totals.reshape(peers, owned)
    picks = picks.reshape(peers, owned)
    group_max = jnp.max(maxima, axis=0)
    group_total = jnp.sum(totals * jnp.exp(maxima - group_max[None, :]), axis=0)
    group_pick = jnp.sum(picks, axis=0)

    def combine_groups(first, second):
        larger = jnp.maximum(first[0], second[0])
        summed = first[1] * jnp.exp(first[0] - larger) + second[1] * jnp.exp(second[0] - larger)
        return (larger, summed, first[2] + second[2])

    overall_max, overall_total, overall_pick = joined_all(
        (group_max, group_total, group_pick), VOCAB, combine_groups
    )
    logprob = overall_pick - (overall_max + jnp.log(overall_total))
    following = from_behind(values[:1], "batch", -1)
    next_values = jnp.concatenate([values[1:], following])
    keeping = 1.0 - segment_end.astype(jnp.float32)
    shaped = rewards - penalty_weight * (logprob - ref_logprob)
    deltas = shaped + discount * next_values * keeping - values
    factors = discount * trace_decay * keeping

    def backward(running, inputs):
        factor, delta = inputs
        accrued = delta + factor * running[0]
        product = factor * running[1]
        return ((accrued, product), (accrued, product))

    finished, outputs = lax.scan(
        backward,
        (jnp.zeros((), jnp.float32), jnp.ones((), jnp.float32)),
        (factors, deltas),
        reverse=True,
    )
    local_adv, products = outputs
    head_adv = local_adv[:1]
    head_prod = products[:1]

    def compose(earlier, later):
        return (later[0] * earlier[0], later[1] + later[0] * earlier[1])

    composed, incoming = prefix(
        (head_prod, head_adv),
        "batch",
        compose,
        (jnp.ones((1,), jnp.float32), jnp.zeros((1,), jnp.float32)),
    )
    advantages = local_adv + products * incoming
    return (logprob, advantages)


def solution(mesh):
    torus = Mesh(mesh.devices.reshape(mesh.shape["batch"], 4, 4), ("batch", "vocab_0", "vocab_1"))
    return jax.shard_map(
        per_device,
        mesh=torus,
        in_specs=(
            P("batch", None),
            P("batch"),
            P(),
            P(None, BATCH_VOCAB),
            P(),
            P("batch"),
            P("batch"),
            P("batch"),
            P("batch"),
        ),
        out_specs=(P("batch"), P("batch")),
        check_vma=False,
    )
```

profile of v0, /device:TPU:1, one launch (start us, length us, event | category | flops | bytes accessed | tf_op | source)
XLA Modules:
  0.0 654.8 jit_solution(7538724835867573216)
XLA Ops:
  7.2 1.0 fusion.7
  8.2 0.7 dynamic_slice.34
  9.0 1.7 fusion.6
  10.8 0.7 reshape.381
  11.5 129.7 %all-gather.6.cloned.1.call-done = bf16[2048,4096]{1,0:T(8,128)(2,1)} async-done(((bf16[8,4096]{1,0:T(8,128)(2,1)}), bf16[2048,4096]{1,0:T(8,128)(2,1)}) %all-gather.6.cloned.1.call-update) | async-done | bytes 16777232 | tf_op jit(solution)/shard_map/all_gather | solution.py:134
  141.2 25.1 %while.36 = (s32[]{:T(128)}, f32[4,512]{1,0:T(4,128)S(1)}, f32[4,512]{1,0:T(4,128)S(1)}, f32[4,512]{1,0:T(4,128)S(1)}, bf16[4,512,4096]{2,1,0:T(8,128)(2,1)}, /*...) while((s32[]{:T(128)}, f32[4,512]{1,0:T(4,128)S(1)}, ...), condition=%wide.region_5.6_spmd.clone, body=%wide.region_1.5_spmd.clone.sunk | while | flops 2102884352 | bytes 10402425 | solution.py:147
  141.2 5.8 fusion.51
  147.5 5.8 fusion.51
  153.7 5.8 fusion.51
  160.0 5.8 fusion.51
  166.9 4.6 all-to-all-start
  172.1 6.4 all-to-all-done
  178.5 3.9 all-to-all-start.1
  182.4 2.1 collective-permute-start
  185.2 4.2 all-to-all-done.1
  189.4 3.9 all-to-all-start.2
  193.4 7.1 %all-to-all-done.2 = f32[16,128,1]{1,2,0:T(1,128)S(1)} async-done(((f32[16,128,1]{1,2,0:T(1,128)}), f32[16,128,1]{1,2,0:T(1,128)S(1)}, u32[]{:S(2)}, u32[]{:S(2)}) %all-to-all-start.2) | async-done | bytes 8224 | tf_op jit(solution)/shard_map/all_to_all | solution.py:160
  200.5 8.5 %all-gather.2 = f32[4,3,128]{2,1,0:T(4,128)S(1)} all-gather(f32[1,3,128]{2,1,0:T(4,128)S(1)} %maximum_bitcast_fusion), channel_id=2, replica_groups=mesh['batch'=16,'vocab_0'=4,'vocab_1'=4] {'vocab_0'}, dimensions={0}, use_global_device_ids=true | all-gather | bytes 7680 | tf_op jit(solution)/shard_map/all_gather | solution.py:23
  209.1 8.1 %all-gather.3 = f32[4,3,128]{2,1,0:T(4,128)S(1)} all-gather(f32[1,3,128]{2,1,0:T(4,128)S(1)} %maximum_bitcast_fusion.1), channel_id=3, replica_groups=mesh['batch'=16,'vocab_0'=4,'vocab_1'=4] {'vocab_1'}, dimensions={0}, use_global_device_ids=true | all-gather | bytes 7680 | tf_op jit(solution)/shard_map/all_gather | solution.py:23
  217.2 1.2 fusion.31
  218.4 408.9 %while.35 = (s32[]{:T(128)}, f32[]{:T(128)}, f32[]{:T(128)}, f32[128]{0:T(128)S(1)}, f32[128]{0:T(128)S(1)}, /*index=5*/f32[128]{0:T(128)S(1)}, f32[128]{0:T(128)S(1)}, s32[]{:T(128)}, s32[]{:T(128)}) while((s32[]{:T(128)}, f32[]{:T(128)}, f32[]{:T(128)}, f32[128]{0:T(128)S(1)}, f32[128]{0:T(128)S(1)}, /*index=5*/f32[128]{0:T(128)S(1)}, ...), condition=%wide.region_10.11_spmd, body=%wide.region_9.10_spmd.sunk | while | flops 6 | bytes 189 | solution.py:191
  219.5 0.6 dynamic_slice.50
  222.7 0.6 dynamic_slice.50
  225.9 0.6 dynamic_slice.50
  229.1 0.6 dynamic_slice.50
  232.3 0.6 dynamic_slice.50
  235.5 0.6 dynamic_slice.50
  238.7 0.6 dynamic_slice.50
  251.5 0.6 dynamic_slice.50
  273.8 0.6 dynamic_slice.50
  293.0 0.6 dynamic_slice.50
  312.2 0.6 dynamic_slice.50
  334.5 0.6 dynamic_slice.50
  353.7 0.6 dynamic_slice.50
  372.9 0.6 dynamic_slice.50
  395.2 0.6 dynamic_slice.50
  414.4 0.6 dynamic_slice.50
  433.6 0.6 dynamic_slice.50
  455.9 0.6 dynamic_slice.50
  475.1 0.6 dynamic_slice.50
  494.3 0.6 dynamic_slice.50
  516.6 0.6 dynamic_slice.50
  535.8 0.6 dynamic_slice.50
  555.0 0.6 dynamic_slice.50
  577.3 0.6 dynamic_slice.50
  596.5 0.6 dynamic_slice.50
  615.7 0.6 dynamic_slice.50
  627.4 15.1 %all_to_all.32 = f32[16,2,1]{1,2,0:T(1,128)S(1)} all-to-all(f32[16,2,1]{1,2,0:T(1,128)S(1)} %broadcast_in_dim.56), channel_id=1, replica_groups=mesh['batch'=16,'vocab_0'=4,'vocab_1'=4] {'batch'}, dimensions={0} | all-to-all | bytes 256 | tf_op jit(solution)/shard_map/all_to_all | solution.py:49
  (562 shorter events, 173.5 us)
Async XLA Ops:
  7.2 1.8 copy-start
  7.2 134.0 %all-gather.6.cloned.1.call-start = ((), (), s32[]{:S(2)}) async-start(), calls=%async_computation.4 | async-start | bytes 16842752 | tf_op jit(solution)/shard_map/all_gather | solution.py:134
  141.2 41.2 %copy-start.1 = (f32[128]{0:T(128)S(1)}, f32[128]{0:T(128)}, u32[]{:S(2)}) copy-start(f32[128]{0:T(128)} %param.18) | copy-start | bytes 1540
  141.2 76.1 %copy-start.2 = (f32[128]{0:T(128)S(1)}, f32[128]{0:T(128)}, u32[]{:S(2)}) copy-start(f32[128]{0:T(128)} %param.19) | copy-start | bytes 1540
  141.2 76.1 %copy-start.3 = (f32[128]{0:T(128)S(1)}, f32[128]{0:T(128)}, u32[]{:S(2)}) copy-start(f32[128]{0:T(128)} %param.20) | copy-start | bytes 1540
  141.2 76.1 %copy-start.4 = (s32[128]{0:T(128)S(1)}, s32[128]{0:T(128)}, u32[]{:S(2)}) copy-start(s32[128]{0:T(128)} %param.21) | copy-start | bytes 1540
  166.9 11.6 %all-to-all-start = ((f32[16,128,1]{1,2,0:T(1,128)}), f32[16,128,1]{1,2,0:T(1,128)S(1)}, u32[]{:S(2)}, u32[]{:S(2)}) async-start(f32[16,128,1]{1,2,0:T(1,128)} %all_to_all.21), calls=%async_computation | async-start | bytes 16384 | tf_op jit(solution)/shard_map/all_to_all | solution.py:158
  178.5 10.9 %all-to-all-start.1 = ((f32[16,128,1]{1,2,0:T(1,128)}), f32[16,128,1]{1,2,0:T(1,128)S(1)}, u32[]{:S(2)}, u32[]{:S(2)}) async-start(f32[16,128,1]{1,2,0:T(1,128)} %all_to_all.23), calls=%async_computation.1 | async-start | bytes 16384 | tf_op jit(solution)/shard_map/all_to_all | solution.py:159
  182.4 34.8 %collective-permute-start = (f32[1]{0:T(128)S(1)}, f32[1]{0:T(128)}, u32[]{:S(2)}, u32[]{:S(2)}) collective-permute-start(f32[1]{0:T(128)S(1)} %bitcast.211), channel_id=1, source_target_pairs={{16,0},{32,16},{48,32},{64,48},{80,64},{96,80},{112,96},{128,112},... | collective-permute-start | bytes 20 | tf_op jit(solution)/shard_map/ppermute | solution.py:44
  189.4 11.0 %all-to-all-start.2 = ((f32[16,128,1]{1,2,0:T(1,128)}), f32[16,128,1]{1,2,0:T(1,128)S(1)}, u32[]{:S(2)}, u32[]{:S(2)}) async-start(f32[16,128,1]{1,2,0:T(1,128)} %all_to_all.25), calls=%async_computation.2 | async-start | bytes 16384 | tf_op jit(solution)/shard_map/all_to_all | solution.py:160
Sparse Core Ops, SparseCore 0:
  11.7 129.4 all-gather.5
where the time goes:
time: 662 us; the launch traced here: 655 us
  loops' own time  227 us (34%)
  local copies, waits for them, and re-layouts  189 us (29%)
  waiting for transfers between devices  147 us (22%)
  blocking collectives  31.8 us (5%)
  matrix products  24.9 us (4%)
  between operations  16 us (2%)
  starting transfers between devices  14.5 us (2%)
    another operation x1, loops' own time, per_device(): lax.scan(backward, (jnp.zeros((), jnp.float32), jnp.ones((), jnp.float32)...  227 us
    dynamic_slice x256, local copies, waits for them, and re-layouts, per_device(): lax.scan(backward, (jnp.zeros((), jnp.float32), jnp.ones((), jnp.float32)...  152 us
    all_gather x1, waiting for transfers between devices, per_device(): gathered = lax.all_gather(normed, BATCH_VOCAB, axis=0, tiled=True)  130 us
    dynamic_update_slice x256, local copies, waits for them, and re-layouts, per_device(): lax.scan(backward, (jnp.zeros((), jnp.float32), jnp.ones((), jnp.float32)...  29.4 us
    dot_general x4, matrix products, score_block(): logits = jnp.dot(rows_block, unembed, preferred_element_type=jnp.float32)  23.2 us
    all_gather x2, blocking collectives, gathered_once(): both, at, found = (lax.all_gather(jnp.concatenate(lines), axis), 0, {})  16.7 us
    all_to_all x1, blocking collectives, from_everyone(): lax.all_to_all(jnp.broadcast_to(shard[None], (length, *shard.shape)), axi...  15.1 us
  transfers between devices with their start and end apart: 5, of which 4 were waited for; matrix products, arithmetic and copies ran while one was open for 0% of the time, Pallas kernels for 0%

commit v1 on v0

--- a/solution.py
+++ b/solution.py
@@ -131,7 +131,9 @@
     own_rows = lax.dynamic_slice_in_dim(hidden, first_row, share, 0)
     own_layers = lax.dynamic_slice_in_dim(exit_layer, first_row, share, 0)
     normed = normalize(own_rows, own_layers, exit_gains)
-    gathered = lax.all_gather(normed, BATCH_VOCAB, axis=0, tiled=True)
+    gathered = jnp.concatenate(
+        lax.all_to_all(jnp.stack([normed] * lax.axis_size(BATCH_VOCAB)), BATCH_VOCAB, 0, 0), axis=0
+    )
     block_rows = 512
     block_count = total_rows // block_rows
 

time: 662 us -> 905 us (1.37)
  waiting for transfers between devices: 147 us -> 382 us
  starting transfers between devices: 14.5 us -> 31.4 us
  between operations: 16 us -> 2.63 us
    all_to_all x0 -> x1, waiting for transfers between devices: none -> 365 us  [per_device(): lax.all_to_all(jnp.stack([normed] * lax.axis_size(BATCH_VOCAB)), BATCH_VO...]
    all_gather x1 -> x0, waiting for transfers between devices: 130 us -> none  [per_device(): gathered = lax.all_gather(normed, BATCH_VOCAB, axis=0, tiled=True)]
    all_to_all x0 -> x1, starting transfers between devices: none -> 16.6 us  [per_device(): lax.all_to_all(jnp.stack([normed] * lax.axis_size(BATCH_VOCAB)), BATCH_VO...]
where the time goes in v1:
time: 905 us; the launch traced here: 898 us
  waiting for transfers between devices  382 us (42%)
  loops' own time  227 us (25%)
  local copies, waits for them, and re-layouts  194 us (21%)
  blocking collectives  31.6 us (3%)
  starting transfers between devices  31.4 us (3%)
  matrix products  24.3 us (3%)
    all_to_all x1, waiting for transfers between devices, per_device(): lax.all_to_all(jnp.stack([normed] * lax.axis_size(BATCH_VOCAB)), BATCH_VO...  365 us
    another operation x1, loops' own time, per_device(): lax.scan(backward, (jnp.zeros((), jnp.float32), jnp.ones((), jnp.float32)...  227 us
    dynamic_slice x256, local copies, waits for them, and re-layouts, per_device(): lax.scan(backward, (jnp.zeros((), jnp.float32), jnp.ones((), jnp.float32)...  152 us
    dynamic_update_slice x256, local copies, waits for them, and re-layouts, per_device(): lax.scan(backward, (jnp.zeros((), jnp.float32), jnp.ones((), jnp.float32)...  29.4 us
    dot_general x4, matrix products, score_block(): logits = jnp.dot(rows_block, unembed, preferred_element_type=jnp.float32)  23.2 us
  transfers between devices with their start and end apart: 5, of which 4 were waited for; matrix products, arithmetic and copies ran while one was open for 0% of the time, Pallas kernels for 0%

profile of v1, /device:TPU:1, one launch (start us, length us, event | category | flops | bytes accessed | tf_op | source)
XLA Modules:
  0.0 897.8 jit_solution(14529282053001577024)
XLA Ops:
  0.7 1.0 fusion.7
  1.7 0.7 dynamic_slice.34
  2.4 1.1 fusion.6
  3.5 6.0 stack.2
  9.5 16.6 %all-to-all-start = ((bf16[256,8,4096]{2,1,0:T(8,128)(2,1)}), bf16[256,8,4096]{2,1,0:T(8,128)(2,1)}, u32[]{:S(2)}, u32[]{:S(2)}) async-start(bf16[256,8,4096]{2,1,0:T(8,128)(2,1)} %stack.2), calls=%async_computation | async-start | bytes 33554432 | tf_op jit(solution)/shard_map/all_to_all | solution.py:135
  26.2 364.6 %all-to-all-done = bf16[256,8,4096]{2,1,0:T(8,128)(2,1)} async-done(((bf16[256,8,4096]{2,1,0:T(8,128)(2,1)}), bf16[256,8,4096]{2,1,0:T(8,128)(2,1)}, u32[]{:S(2)}, u32[]{:S(2)}) %all-to-all-start) | async-done | bytes 16777248 | tf_op jit(solution)/shard_map/all_to_all | solution.py:135
  390.8 25.1 %while.36 = (s32[]{:T(128)}, f32[4,512]{1,0:T(4,128)S(1)}, f32[4,512]{1,0:T(4,128)S(1)}, f32[4,512]{1,0:T(4,128)S(1)}, bf16[4,512,4096]{2,1,0:T(8,128)(2,1)}, /*...) while((s32[]{:T(128)}, f32[4,512]{1,0:T(4,128)S(1)}, ...), condition=%wide.region_5.6_spmd.clone, body=%wide.region_1.5_spmd.clone.sunk | while | flops 2102884352 | bytes 10402425 | solution.py:149
  390.8 5.8 fusion.51
  397.1 5.8 fusion.51
  403.4 5.8 fusion.51
  409.7 5.8 fusion.51
  416.5 4.9 all-to-all-start.1
  422.0 6.4 all-to-all-done.1
  428.4 3.9 all-to-all-start.2
  432.3 2.1 collective-permute-start
  435.2 4.2 all-to-all-done.2
  439.4 3.9 all-to-all-start.3
  443.3 7.1 all-to-all-done.3
  450.4 8.4 all-gather.2
  458.9 8.1 all-gather.3
  467.0 1.2 fusion.31
  468.2 408.9 %while.35 = (s32[]{:T(128)}, f32[]{:T(128)}, f32[]{:T(128)}, f32[128]{0:T(128)S(1)}, f32[128]{0:T(128)S(1)}, /*index=5*/f32[128]{0:T(128)S(1)}, f32[128]{0:T(128)S(1)}, s32[]{:T(128)}, s32[]{:T(128)}) while((s32[]{:T(128)}, f32[]{:T(128)}, f32[]{:T(128)}, f32[128]{0:T(128)S(1)}, f32[128]{0:T(128)S(1)}, /*index=5*/f32[128]{0:T(128)S(1)}, ...), condition=%wide.region_10.11_spmd, body=%wide.region_9.10_spmd.sunk | while | flops 6 | bytes 189 | solution.py:193
  469.3 0.6 dynamic_slice.50
  472.5 0.6 dynamic_slice.50
  475.7 0.6 dynamic_slice.50
  478.9 0.6 dynamic_slice.50
  482.1 0.6 dynamic_slice.50
  488.5 0.6 dynamic_slice.50
  507.7 0.6 dynamic_slice.50
  530.0 0.6 dynamic_slice.50
  549.2 0.6 dynamic_slice.50
  568.4 0.6 dynamic_slice.50
  590.7 0.6 dynamic_slice.50
  609.9 0.6 dynamic_slice.50
  629.1 0.6 dynamic_slice.50
  651.4 0.6 dynamic_slice.50
  670.6 0.6 dynamic_slice.50
  689.8 0.6 dynamic_slice.50
  712.1 0.6 dynamic_slice.50
  731.3 0.6 dynamic_slice.50
  750.5 0.6 dynamic_slice.50
  772.8 0.6 dynamic_slice.50
  792.0 0.6 dynamic_slice.50
  811.2 0.6 dynamic_slice.50
  833.5 0.6 dynamic_slice.50
  852.7 0.6 dynamic_slice.50
  871.9 0.6 dynamic_slice.50
  877.2 15.1 %all_to_all.37 = f32[16,2,1]{1,2,0:T(1,128)S(1)} all-to-all(f32[16,2,1]{1,2,0:T(1,128)S(1)} %broadcast_in_dim.56), channel_id=1, replica_groups=mesh['batch'=16,'vocab_0'=4,'vocab_1'=4] {'batch'}, dimensions={0} | all-to-all | bytes 256 | tf_op jit(solution)/shard_map/all_to_all | solution.py:49
  (564 shorter events, 174.0 us)
Async XLA Ops:
  0.6 1.8 copy-start
  9.5 16.7 %copy-start.1 = (s32[2048]{0:T(1024)S(1)}, s32[2048]{0:T(1024)}, u32[]{:S(2)}) copy-start(s32[2048]{0:T(1024)} %param.17) | copy-start | bytes 24580
  9.5 381.3 %all-to-all-start = ((bf16[256,8,4096]{2,1,0:T(8,128)(2,1)}), bf16[256,8,4096]{2,1,0:T(8,128)(2,1)}, u32[]{:S(2)}, u32[]{:S(2)}) async-start(bf16[256,8,4096]{2,1,0:T(8,128)(2,1)} %stack.2), calls=%async_computation | async-start | bytes 33554432 | tf_op jit(solution)/shard_map/all_to_all | solution.py:135
  390.8 41.5 %copy-start.2 = (f32[128]{0:T(128)S(1)}, f32[128]{0:T(128)}, u32[]{:S(2)}) copy-start(f32[128]{0:T(128)} %param.18) | copy-start | bytes 1540
  390.8 76.2 %copy-start.3 = (f32[128]{0:T(128)S(1)}, f32[128]{0:T(128)}, u32[]{:S(2)}) copy-start(f32[128]{0:T(128)} %param.19) | copy-start | bytes 1540
  390.8 76.2 %copy-start.4 = (f32[128]{0:T(128)S(1)}, f32[128]{0:T(128)}, u32[]{:S(2)}) copy-start(f32[128]{0:T(128)} %param.20) | copy-start | bytes 1540
  390.8 76.2 %copy-start.5 = (s32[128]{0:T(128)S(1)}, s32[128]{0:T(128)}, u32[]{:S(2)}) copy-start(s32[128]{0:T(128)} %param.21) | copy-start | bytes 1540
  416.5 11.9 %all-to-all-start.1 = ((f32[16,128,1]{1,2,0:T(1,128)}), f32[16,128,1]{1,2,0:T(1,128)S(1)}, u32[]{:S(2)}, u32[]{:S(2)}) async-start(f32[16,128,1]{1,2,0:T(1,128)} %all_to_all.25), calls=%async_computation.1 | async-start | bytes 16384 | tf_op jit(solution)/shard_map/all_to_all | solution.py:160
  428.4 10.9 %all-to-all-start.2 = ((f32[16,128,1]{1,2,0:T(1,128)}), f32[16,128,1]{1,2,0:T(1,128)S(1)}, u32[]{:S(2)}, u32[]{:S(2)}) async-start(f32[16,128,1]{1,2,0:T(1,128)} %all_to_all.27), calls=%async_computation.2 | async-start | bytes 16384 | tf_op jit(solution)/shard_map/all_to_all | solution.py:161
  432.3 34.7 %collective-permute-start = (f32[1]{0:T(128)S(1)}, f32[1]{0:T(128)}, u32[]{:S(2)}, u32[]{:S(2)}) collective-permute-start(f32[1]{0:T(128)S(1)} %bitcast.211), channel_id=1, source_target_pairs={{16,0},{32,16},{48,32},{64,48},{80,64},{96,80},{112,96},{128,112},... | collective-permute-start | bytes 20 | tf_op jit(solution)/shard_map/ppermute | solution.py:44
  439.4 11.0 %all-to-all-start.3 = ((f32[16,128,1]{1,2,0:T(1,128)}), f32[16,128,1]{1,2,0:T(1,128)S(1)}, u32[]{:S(2)}, u32[]{:S(2)}) async-start(f32[16,128,1]{1,2,0:T(1,128)} %all_to_all.29), calls=%async_computation.3 | async-start | bytes 16384 | tf_op jit(solution)/shard_map/all_to_all | solution.py:162
